TPU v7x, 32 devices: a whole 2x2x4 slice. The times are simulated.
32 devices in a mesh: row: 8 (over z, y), expert: 4 (over x, core).
Axes of the slice: x: 2, y: 2, z: 4, core: 2. Of those that a mesh axis runs over, the one named last changes fastest.
Arguments:
- base: bfloat16 [8, 7168, 2048], P('expert', 'row'), may hold values from -6 to 6
- left_factors: bfloat16 [8, 7168, 64], P('expert', None, 'row'), may hold values from -6 to 6
- right_factors: bfloat16 [8, 64, 2048], P('expert', None, 'row'), may hold values from -0.75 to 0.75
- expert_adapter_scale: float32 [8], P('expert'), may hold values from 0.5 to 2
- placement: int32 [8], P('expert'), may hold values from 0 to 3, as said below
Outputs:
- serving: bfloat16 [8, 7168, 2048], P('expert', None, 'row')
Inputs may be any that keep to these rules, and one draw needn't show every extreme that they name: `placement`: expert g * 2 + j is placed on (g + o_j) mod (4) for one offset o_j per slot j, the same for every g; the offsets of slots 0 and 1 add up to 3.
All inputs are finite; a program needn't handle non-finite values.
Results may differ from a plain program's by a relative error of at most 0.001.
Values may be sent and summed in bfloat16 or wider, within the bound.
A program may use at most 64 MiB of HBM per device.

v0:
```python
import functools

import jax
import jax.numpy as jnp
from jax import lax
from jax.experimental import pallas as pl
from jax.experimental.pallas import tpu as pltpu
from jax.sharding import PartitionSpec as P

MESH = pl.DeviceIdType.MESH
WINDOW = 8


def piece_order(rows):
    half = rows // 2
    near = sorted(range(half), key=lambda m: (m == 0, m != half // 2, m))
    return [m for pair in zip(range(half, rows), near) for m in pair]


def exchange_kernel(dist, groups, rows, base, left, right, scale, got, left_all, right_got, scale_got,
                    bounce, send, recv, lsend, lrecv, ssend, srecv, own):
    r, g = lax.axis_index("row"), lax.axis_index("expert")
    slots, height = base.shape[0], base.shape[1]
    width = base.shape[2] // rows
    to = [lax.rem(g + d, groups) for d in dist]

    barrier = pltpu.get_barrier_semaphore()
    steps = sorted({d for d in dist} | {(groups - d) % groups for d in dist} | {0})
    for e in steps:
        for m in range(rows):
            if e == 0 and m == 0:
                continue
            pl.semaphore_signal(barrier, inc=1, device_id={"row": r ^ m, "expert": lax.rem(g + e, groups)},
                                device_id_type=MESH)
    pl.semaphore_wait(barrier, len(steps) * rows - 1)

    def remote(src, dst, s, t, row, expert):
        return pltpu.make_async_remote_copy(src_ref=src, dst_ref=dst, send_sem=s, recv_sem=t,
                                            device_id={"row": row, "expert": expert}, device_id_type=MESH)

    first = []
    for j in range(slots):
        for src, dst, s, t in (
            (left.at[j], left_all.at[j, r], lsend.at[j, 0], lrecv.at[j, 0]),
            (right.at[j], right_got.at[j], ssend.at[j, 0], srecv.at[j, 0]),
            (scale.at[j], scale_got.at[j], ssend.at[j, 1], srecv.at[j, 1]),
        ):
            if dist[j] == 0:
                copy = pltpu.make_async_copy(src, dst, t)
            else:
                copy = remote(src, dst, s, t, r, to[j])
            copy.start()
            first.append(copy)

    def left_round(mask, held):
        copies = []
        for s in held:
            for j in range(slots):
                piece = left_all.at[j, r ^ s]
                copy = remote(piece, piece, lsend.at[j, mask | s], lrecv.at[j, mask | s], r ^ mask, g)
                copy.start()
                copies.append(copy)
        return copies

    rounds = []
    mask, held = rows // 2, [0]
    while mask:
        rounds.append((mask, list(held)))
        held += [s | mask for s in held]
        mask //= 2

    pieces = [(m, j) for m in piece_order(rows) for j in range(slots)]
    at = {1 + i * (len(pieces) // len(rounds)): i for i in range(len(rounds))}
    pending, sent, waiting = [], [], first
    for k, (m, j) in enumerate(pieces):
        if k in at:
            for copy in waiting:
                copy.wait()
            waiting = left_round(*rounds[at[k]])
        if len(pending) >= WINDOW:
            pending.pop(0).wait_send()
        c = r ^ m
        src = base.at[j, :, pl.ds(pl.multiple_of(c * width, width), width)]
        if m == 0 and dist[j] == 0:
            copy = pltpu.make_async_copy(src, bounce, own)
            copy.start()
            copy.wait()
            copy = pltpu.make_async_copy(bounce, got.at[j, r], own)
            copy.start()
            last = copy
            sent.append(copy.wait)
        else:
            copy = remote(src, got.at[j, r], send.at[j, m], recv.at[j, m], c, to[j])
            copy.start()
            pending.append(copy)
            sent.append(copy.wait_recv)
    for copy in waiting:
        copy.wait()
    for copy in pending:
        copy.wait_send()
    for wait in sent:
        wait()


def exchange(first, groups, rows, base, left, right, scale):
    dist = (first, groups - 1 - first)
    slots, height, total = base.shape
    width = total // rows
    rank, model = left.shape[1:]
    anywhere = pl.BlockSpec(memory_space=pl.ANY)
    dma = pltpu.SemaphoreType.DMA
    return pl.pallas_call(
        functools.partial(exchange_kernel, dist, groups, rows),
        out_shape=(
            jax.ShapeDtypeStruct((slots, rows, height, width), base.dtype),
            jax.ShapeDtypeStruct((slots, rows, rank, model), left.dtype),
            jax.ShapeDtypeStruct(right.shape, right.dtype),
            jax.ShapeDtypeStruct(scale.shape, scale.dtype),
        ),
        in_specs=[anywhere] * 4,
        out_specs=[anywhere] * 4,
        scratch_shapes=[
            pltpu.VMEM((height, width), base.dtype),
            dma((slots, rows)), dma((slots, rows)),
            dma((slots, rows)), dma((slots, rows)),
            dma((slots, 2)), dma((slots, 2)),
            dma,
        ],
        compiler_params=pltpu.CompilerParams(collective_id=first, has_side_effects=True),
        name=f"exchange_{first}",
    )(base, left, right, scale)


def merge_kernel(base, left, right, scale, out):
    delta = lax.dot_general(left[0], right[0], (((0,), (0,)), ((), ())), preferred_element_type=jnp.float32)
    out[0] = (base[0].astype(jnp.float32) + scale[0, 0:1, 0:1] * delta).astype(out.dtype)


def merge(base, left, right, scale):
    slots, model, width = base.shape
    rank = left.shape[1]
    block = next(b for b in (1024, 512, 256, 128) if model % b == 0)
    return pl.pallas_call(
        merge_kernel,
        grid=(slots, model // block),
        in_specs=[
            pl.BlockSpec((1, block, width), lambda j, i: (j, i, 0)),
            pl.BlockSpec((1, rank, block), lambda j, i: (j, 0, i)),
            pl.BlockSpec((1, rank, width), lambda j, i: (j, 0, 0)),
            pl.BlockSpec((1,) + scale.shape[1:], lambda j, i: (j, 0, 0)),
        ],
        out_specs=pl.BlockSpec((1, block, width), lambda j, i: (j, i, 0)),
        out_shape=jax.ShapeDtypeStruct(base.shape, base.dtype),
        compiler_params=pltpu.CompilerParams(dimension_semantics=("arbitrary", "arbitrary")),
        name="merge",
    )(base, left, right, scale)


def local(groups, rows, base, left_factors, right_factors, expert_adapter_scale, placement):
    first = jnp.mod(placement[0] - lax.axis_index("expert"), groups)
    slots = base.shape[0]
    left = jnp.swapaxes(left_factors, 1, 2)
    scale = jnp.broadcast_to(expert_adapter_scale[:, None, None], (slots, 8, 128))
    got, left_all, right, scale = lax.switch(
        first,
        [functools.partial(exchange, o, groups, rows) for o in range(groups)],
        base, left, right_factors, scale,
    )
    model = left.shape[2]
    return merge(
        got.reshape(slots, model, got.shape[3]),
        left_all.reshape(slots, -1, model),
        right,
        scale,
    )


def solution(mesh):
    placed = (
        P("expert", "row", None),
        P("expert", None, "row"),
        P("expert", None, "row"),
        P("expert"),
        P("expert"),
    )
    return jax.shard_map(
        functools.partial(local, mesh.shape["expert"], mesh.shape["row"]),
        mesh=mesh, in_specs=placed, out_specs=P("expert", None, "row"), check_vma=False,
    )
```

profile of v0, /device:TPU:9, one launch (start us, length us, event | category | flops | bytes accessed | tf_op | source)
XLA Modules:
  0.0 189.9 jit_solution(10290856091273550538)
XLA Ops:
  0.7 176.8 %conditional.1 = ((bf16[2,8,896,256]{3,2,1,0:T(8,128)(2,1)}, bf16[2,8,8,7168]{3,2,1,0:T(8,128)(2,1)S(1)}, bf16[2,64,256]{2,1,0:T(8,128)(2,1)S(1)}, f32[2,8,128]{2,1,0:T(8,128)S(1)})) conditional(s32[]{:T(128)} %clamp.3, (bf16[2,896,2048]{2,1,0:T(8,128)(2,1)}, bf16[2,8,7168]{2,1,0:T(8,128)(2,1)}, ...), branch_computations={%region_0.1_spmd, %region_1.2_spmd, %region_2.3_spmd, %region_3.4_... | conditional | bytes 8208 | solution.py:164
  0.7 1.3 broadcast_in_dim.9.scale
  2.0 175.4 %exchange_2.1 = (bf16[2,8,896,256]{3,2,1,0:T(8,128)(2,1)}, bf16[2,8,8,7168]{3,2,1,0:T(8,128)(2,1)S(1)}, bf16[2,64,256]{2,1,0:T(8,128)(2,1)S(1)}, f32[2,8,128]{2,1,0:T(8,128)S(1)}) custom-call(bf16[2,896,2048]{2,1,0:T(8,128)(2,1)} %get-tuple-element.116.base, bf16[2,8,7168]{2,1,0:T(8,128)(2,1)} %get-tuple-element.69.left, ...), custom_call_target="tpu_custom_call" | custom-call | tf_op jit(solution)/shard_map/cond/branch_2_fun/exchange_2/pallas_call | solution.py:112
  177.4 12.4 %merge.1 = bf16[2,7168,256]{2,1,0:T(8,128)(2,1)} custom-call(bf16[2,7168,256]{2,1,0:T(8,128)(2,1)} %bitcast.5, bf16[2,64,7168]{2,1,0:T(8,128)(2,1)S(1)} %bitcast.10, bf16[2,64,256]{2,1,0:T(8,128)(2,1)S(1)} %get-tuple-element.134.right, f32[2,8,128]{2,1,0:T(8,128)S(1)} %get-tuple-element.133.scale), custom_call_target="tpu_custom_call" | custom-call | tf_op jit(solution)/shard_map/merge/pallas_call | solution.py:143
where the time goes:
time: 189 us; the launch traced here: 190 us
  Pallas kernels  188 us (99%)
    pallas_call x1, Pallas kernels, exchange(): pl.pallas_call(functools.partial(exchange_kernel, dist, groups, rows), ou...  175 us
    pallas_call x1, Pallas kernels, merge(): pl.pallas_call(merge_kernel, grid=(slots, model // block), in_specs=[pl.B...  12.4 us

commit v1 on v0

v1 whole, which is shorter than its diff:
```python
import functools

import jax
import jax.numpy as jnp
from jax import lax
from jax.experimental import pallas as pl
from jax.experimental.pallas import tpu as pltpu
from jax.sharding import PartitionSpec as P

MESH = pl.DeviceIdType.MESH
WINDOW = 8
LANES = 128


def piece_order(rows):
    half = rows // 2
    return [m for q in range(half) for m in (half + q, (half // 2 + q) % half)]


def exchange_kernel(dist, groups, rows, base, left, right, scale, out, got, left_all, right_got, scale_got,
                    send, recv, lsend, lrecv, ssend, srecv, osem):
    r, g = lax.axis_index("row"), lax.axis_index("expert")
    slots, _, height, width = got.shape
    to = [lax.rem(g + d, groups) for d in dist]

    barrier = pltpu.get_barrier_semaphore()
    steps = sorted({d for d in dist} | {(groups - d) % groups for d in dist} | {0})
    for e in steps:
        for m in range(rows):
            if e == 0 and m == 0:
                continue
            pl.semaphore_signal(barrier, inc=1, device_id={"row": r ^ m, "expert": lax.rem(g + e, groups)},
                                device_id_type=MESH)
    pl.semaphore_wait(barrier, len(steps) * rows - 1)

    def remote(src, dst, s, t, row, expert):
        return pltpu.make_async_remote_copy(src_ref=src, dst_ref=dst, send_sem=s, recv_sem=t,
                                            device_id={"row": row, "expert": expert}, device_id_type=MESH)

    first = []
    for j in range(slots):
        for src, dst, s, t in (
            (left.at[j], left_all.at[j, r], lsend.at[j, 0], lrecv.at[j, 0]),
            (right.at[j], right_got.at[j], ssend.at[j, 0], srecv.at[j, 0]),
            (scale.at[j], scale_got.at[j], ssend.at[j, 1], srecv.at[j, 1]),
        ):
            if dist[j] == 0:
                copy = pltpu.make_async_copy(src, dst, t)
            else:
                copy = remote(src, dst, s, t, r, to[j])
            copy.start()
            first.append(copy)

    def left_round(mask, held):
        copies = []
        for s in held:
            for j in range(slots):
                piece = left_all.at[j, r ^ s]
                copy = remote(piece, piece, lsend.at[j, mask | s], lrecv.at[j, mask | s], r ^ mask, g)
                copy.start()
                copies.append(copy)
        return copies

    rounds = []
    mask, held = rows // 2, [0]
    while mask:
        rounds.append((mask, list(held)))
        held += [s | mask for s in held]
        mask //= 2

    pieces = [(m, j) for m in piece_order(rows) for j in range(slots)]
    at = {1 + i * (len(pieces) // len(rounds)): i for i in range(len(rounds))}
    pending, waiting = [], first
    for k, (m, j) in enumerate(pieces):
        if k in at:
            for copy in waiting:
                copy.wait()
            waiting = left_round(*rounds[at[k]])
        if len(pending) >= WINDOW:
            pending.pop(0).wait_send()
        c = r ^ m
        src = base.at[j, :, pl.ds(pl.multiple_of(c * width, width), width)]
        if m == 0 and dist[j] == 0:
            pltpu.make_async_copy(src, got.at[j, r], recv.at[j, 0]).start()
        else:
            copy = remote(src, got.at[j, r], send.at[j, m], recv.at[j, m], c, to[j])
            copy.start()
            pending.append(copy)
    for copy in waiting:
        copy.wait()

    unit = next(u for u in (1, 2, 4, 8) if u * height % LANES == 0)
    half = rows // 2
    turns = rows * slots // unit

    def place(t):
        q, f, j = t // (2 * slots) * unit, t // slots % 2, t % slots
        m = (1 - f) * (half + q) + f * ((half // 2 + q) % half)
        return m, j, (r ^ m) // unit * unit

    def written(t):
        m, j, row = place(t)
        rows_of = pl.ds(pl.multiple_of(row, unit), unit)
        return pltpu.make_async_copy(got.at[j, rows_of], out.at[j, rows_of], osem.at[t])

    def turn(t, carry):
        m, j, row = place(t)
        for u in range(unit):
            block = got.at[j, r ^ (m + u)]
            remote(block, block, send.at[j, m + u], recv.at[j, m + u], r ^ 1, g).wait_recv()
        rank_all = left_all.shape[1] * left_all.shape[2]
        columns = pl.ds(pl.multiple_of(row * height, LANES), unit * height)
        a = left_all[j, :, :, columns].reshape(rank_all, unit * height)
        delta = lax.dot_general(a, right_got[j], (((0,), (0,)), ((), ())), preferred_element_type=jnp.float32)
        weight = scale_got[j, 0:1, 0:1]
        for u in range(unit):
            part = delta[u * height:(u + 1) * height]
            got[j, row + u] = (got[j, row + u].astype(jnp.float32) + weight * part).astype(got.dtype)
        written(t).start()
        return carry

    lax.fori_loop(0, turns, turn, 0)
    for copy in pending:
        copy.wait_send()

    def settle(t, carry):
        written(t).wait()
        return carry

    lax.fori_loop(0, turns, settle, 0)


def exchange(first, groups, rows, base, left, right, scale):
    dist = (first, groups - 1 - first)
    slots, height, total = base.shape
    width = total // rows
    rank, model = left.shape[1:]
    anywhere = pl.BlockSpec(memory_space=pl.ANY)
    dma = pltpu.SemaphoreType.DMA
    return pl.pallas_call(
        functools.partial(exchange_kernel, dist, groups, rows),
        out_shape=jax.ShapeDtypeStruct((slots, rows, height, width), base.dtype),
        in_specs=[anywhere] * 4,
        out_specs=anywhere,
        scratch_shapes=[
            pltpu.VMEM((slots, rows, height, width), base.dtype),
            pltpu.VMEM((slots, rows, rank, model), left.dtype),
            pltpu.VMEM(right.shape, right.dtype),
            pltpu.VMEM(scale.shape, scale.dtype),
            dma((slots, rows)), dma((slots, rows)),
            dma((slots, rows)), dma((slots, rows)),
            dma((slots, 2)), dma((slots, 2)),
            dma((slots * rows,)),
        ],
        compiler_params=pltpu.CompilerParams(collective_id=first, has_side_effects=True),
        name=f"exchange_{first}",
    )(base, left, right, scale)


def local(groups, rows, base, left_factors, right_factors, expert_adapter_scale, placement):
    first = jnp.mod(placement[0] - lax.axis_index("expert"), groups)
    slots = base.shape[0]
    left = jnp.swapaxes(left_factors, 1, 2)
    scale = jnp.broadcast_to(expert_adapter_scale[:, None, None], (slots, 8, 128))
    served = lax.switch(
        first,
        [functools.partial(exchange, o, groups, rows) for o in range(groups)],
        base, left, right_factors, scale,
    )
    return served.reshape(slots, left.shape[2], served.shape[3])


def solution(mesh):
    placed = (
        P("expert", "row", None),
        P("expert", None, "row"),
        P("expert", None, "row"),
        P("expert"),
        P("expert"),
    )
    return jax.shard_map(
        functools.partial(local, mesh.shape["expert"], mesh.shape["row"]),
        mesh=mesh, in_specs=placed, out_specs=P("expert", None, "row"), check_vma=False,
    )
```

time: 189 us -> 194 us (1.026)
  local copies, waits for them, and re-layouts: 1.33 us -> 7.93 us
  Pallas kernels: 188 us -> 185 us
    pallas_call x1 -> x0, Pallas kernels: 12.4 us -> none  [merge(): pl.pallas_call(merge_kernel, grid=(slots, model // block), in_specs=[pl.B...]
    pallas_call x1, Pallas kernels: 175 us -> 185 us  [exchange(): pl.pallas_call(functools.partial(exchange_kernel, dist, groups, rows), ou...]
    unnamed x0 -> x1, local copies, waits for them, and re-layouts: none -> 6.6 us
where the time goes in v1:
time: 194 us
  Pallas kernels  185 us (95%)
  local copies, waits for them, and re-layouts  7.93 us (4%)
    pallas_call x1, Pallas kernels, exchange(): pl.pallas_call(functools.partial(exchange_kernel, dist, groups, rows), ou...  185 us
    unnamed x1, local copies, waits for them, and re-layouts  6.6 us

profile of v1, /device:TPU:9, one launch (start us, length us, event | category | flops | bytes accessed | tf_op | source)
XLA Modules:
  0.0 194.0 jit_solution(13411491493611942803)
XLA Ops:
  0.7 186.7 %conditional.1 = (bf16[2,7168,256]{2,1,0:T(8,128)(2,1)}) conditional(s32[]{:T(128)} %clamp.3, (bf16[2,896,2048]{2,1,0:T(8,128)(2,1)}, bf16[2,8,7168]{2,1,0:T(8,128)(2,1)}, bf16[2,64,256]{2,1,0:T(8,128)(2,1)}, f32[2]{0:T(128)}) %tuple.30, (bf16[2,896,2048]{2,1,0:T(8,128)(2,1)}, bf16[2,8,7168]{2,1,0:T(8,128)(2,1)}, ...), branch_computations={%region_0.1_spmd, %region_1.2_spmd, %region_2.3_spmd, %region_3.4_... | conditional | bytes 8208 | solution.py:165
  0.7 1.3 broadcast_in_dim.8.scale
  2.0 185.3 %exchange_1.1 = bf16[2,8,896,256]{3,2,1,0:T(8,128)(2,1)} custom-call(bf16[2,896,2048]{2,1,0:T(8,128)(2,1)} %get-tuple-element.73.base, bf16[2,8,7168]{2,1,0:T(8,128)(2,1)} %get-tuple-element.48.left, bf16[2,64,256]{2,1,0:T(8,128)(2,1)} %get-tuple-element.77.right, f32[2,8,128]{2,1,0:T(8,128)} %broadcast_in_dim.8.scale), custom_call_target="tpu_custom_call" | custom-call | tf_op jit(solution)/shard_map/cond/branch_1_fun/exchange_1/pallas_call | solution.py:140
  187.4 6.6 %copy.27 = bf16[2,7168,256]{2,1,0:T(8,128)(2,1)} copy(bf16[2,7168,256]{2,1,0:T(8,128)(2,1)} %get-tuple-element.59) | data formatting | bytes 14680064

commit v2 on v1

--- a/solution.py
+++ b/solution.py
@@ -12,9 +12,22 @@
 LANES = 128
 
 
-def piece_order(rows):
+def unit_of(height):
+    return next(u for u in (1, 2, 4, 8) if u * height % LANES == 0)
+
+
+def near_turn(q, half):
+    quarter = half // 2
+    return (q + q // quarter) % half + quarter * (1 - (q + half - 1) // half)
+
+
+def piece_order(rows, unit):
     half = rows // 2
-    return [m for q in range(half) for m in (half + q, (half // 2 + q) % half)]
+    order = []
+    for q in range(half // unit):
+        for m in (half + q * unit, near_turn(q, half // unit) * unit):
+            order += range(m, m + unit)
+    return order
 
 
 def exchange_kernel(dist, groups, rows, base, left, right, scale, out, got, left_all, right_got, scale_got,
@@ -68,7 +81,7 @@
         held += [s | mask for s in held]
         mask //= 2
 
-    pieces = [(m, j) for m in piece_order(rows) for j in range(slots)]
+    pieces = [(m, j) for m in piece_order(rows, unit_of(height)) for j in range(slots)]
     at = {1 + i * (len(pieces) // len(rounds)): i for i in range(len(rounds))}
     pending, waiting = [], first
     for k, (m, j) in enumerate(pieces):
@@ -89,13 +102,13 @@
     for copy in waiting:
         copy.wait()
 
-    unit = next(u for u in (1, 2, 4, 8) if u * height % LANES == 0)
+    unit = unit_of(height)
     half = rows // 2
     turns = rows * slots // unit
 
     def place(t):
-        q, f, j = t // (2 * slots) * unit, t // slots % 2, t % slots
-        m = (1 - f) * (half + q) + f * ((half // 2 + q) % half)
+        q, f, j = t // (2 * slots), t // slots % 2, t % slots
+        m = (1 - f) * (half + q * unit) + f * near_turn(q, half // unit) * unit
         return m, j, (r ^ m) // unit * unit
 
     def written(t):

time: 194 us -> 185 us (0.954)
  Pallas kernels: 185 us -> 176 us
    pallas_call x1, Pallas kernels: 185 us -> 176 us  [exchange(): pl.pallas_call(functools.partial(exchange_kernel, dist, groups, rows), ou...]
where the time goes in v2:
time: 185 us
  Pallas kernels  176 us (95%)
  local copies, waits for them, and re-layouts  7.93 us (4%)
    pallas_call x1, Pallas kernels, exchange(): pl.pallas_call(functools.partial(exchange_kernel, dist, groups, rows), ou...  176 us
    unnamed x1, local copies, waits for them, and re-layouts  6.6 us

profile of v2, /device:TPU:9, one launch (start us, length us, event | category | flops | bytes accessed | tf_op | source)
XLA Modules:
  0.0 184.7 jit_solution(503684274350086509)
XLA Ops:
  0.7 177.4 %conditional.1 = (bf16[2,7168,256]{2,1,0:T(8,128)(2,1)}) conditional(s32[]{:T(128)} %clamp.3, (bf16[2,896,2048]{2,1,0:T(8,128)(2,1)}, bf16[2,8,7168]{2,1,0:T(8,128)(2,1)}, bf16[2,64,256]{2,1,0:T(8,128)(2,1)}, f32[2]{0:T(128)}) %tuple.30, (bf16[2,896,2048]{2,1,0:T(8,128)(2,1)}, bf16[2,8,7168]{2,1,0:T(8,128)(2,1)}, ...), branch_computations={%region_0.1_spmd, %region_1.2_spmd, %region_2.3_spmd, %region_3.4_... | conditional | bytes 8208 | solution.py:178
  0.7 1.3 broadcast_in_dim.3.scale
  2.0 176.0 %exchange_0.1 = bf16[2,8,896,256]{3,2,1,0:T(8,128)(2,1)} custom-call(bf16[2,896,2048]{2,1,0:T(8,128)(2,1)} %get-tuple-element.72.base, bf16[2,8,7168]{2,1,0:T(8,128)(2,1)} %get-tuple-element.44.left, bf16[2,64,256]{2,1,0:T(8,128)(2,1)} %get-tuple-element.76.right, f32[2,8,128]{2,1,0:T(8,128)} %broadcast_in_dim.3.scale), custom_call_target="tpu_custom_call" | custom-call | tf_op jit(solution)/shard_map/cond/branch_0_fun/exchange_0/pallas_call | solution.py:153
  178.1 6.6 %copy.27 = bf16[2,7168,256]{2,1,0:T(8,128)(2,1)} copy(bf16[2,7168,256]{2,1,0:T(8,128)(2,1)} %get-tuple-element.59) | data formatting | bytes 14680064

commit v3 on v2

--- a/solution.py
+++ b/solution.py
@@ -170,6 +170,36 @@
     )(base, left, right, scale)
 
 
+def copy_out_kernel(chunks, x, y, held, rsem, wsem):
+    size = x.shape[1] // chunks
+    reads, writes = [], []
+    for j in range(x.shape[0]):
+        for i in range(chunks):
+            here = pl.ds(i * size, size)
+            reads.append(pltpu.make_async_copy(x.at[j, here], held.at[j, here], rsem.at[j, i]))
+            writes.append(pltpu.make_async_copy(held.at[j, here], y.at[j, here], wsem.at[j, i]))
+    for copy in reads:
+        copy.start()
+    for read, write in zip(reads, writes):
+        read.wait()
+        write.start()
+    for copy in writes:
+        copy.wait()
+
+
+def copy_out(x, chunks=7):
+    dma = pltpu.SemaphoreType.DMA
+    anywhere = pl.BlockSpec(memory_space=pl.ANY)
+    return pl.pallas_call(
+        functools.partial(copy_out_kernel, chunks),
+        out_shape=jax.ShapeDtypeStruct(x.shape, x.dtype),
+        in_specs=[anywhere],
+        out_specs=anywhere,
+        scratch_shapes=[pltpu.VMEM(x.shape, x.dtype), dma((x.shape[0], chunks)), dma((x.shape[0], chunks))],
+        name="copy_out",
+    )(x)
+
+
 def local(groups, rows, base, left_factors, right_factors, expert_adapter_scale, placement):
     first = jnp.mod(placement[0] - lax.axis_index("expert"), groups)
     slots = base.shape[0]
@@ -180,7 +210,7 @@
         [functools.partial(exchange, o, groups, rows) for o in range(groups)],
         base, left, right_factors, scale,
     )
-    return served.reshape(slots, left.shape[2], served.shape[3])
+    return copy_out(served.reshape(slots, left.shape[2], served.shape[3]))
 
 
 def solution(mesh):

time: 185 us -> 184 us (level)
  local copies, waits for them, and re-layouts: 7.93 us -> 0.73 us
  Pallas kernels: 176 us -> 183 us
    unnamed x1 -> x0, local copies, waits for them, and re-layouts: 6.6 us -> none
    pallas_call x0 -> x1, Pallas kernels: none -> 5.97 us  [copy_out(): pl.pallas_call(functools.partial(copy_out_kernel, chunks), out_shape=jax....]
where the time goes in v3:
time: 184 us; the launch traced here: 185 us
  Pallas kernels  183 us (99%)
    pallas_call x1, Pallas kernels, exchange(): pl.pallas_call(functools.partial(exchange_kernel, dist, groups, rows), ou...  177 us
    pallas_call x1, Pallas kernels, copy_out(): pl.pallas_call(functools.partial(copy_out_kernel, chunks), out_shape=jax....  5.97 us

profile of v3, /device:TPU:9, one launch (start us, length us, event | category | flops | bytes accessed | tf_op | source)
XLA Modules:
  0.0 184.6 jit_solution(17835697948100511039)
XLA Ops:
  0.7 0.7 broadcast_in_dim.2
  1.4 177.3 %conditional.1 = (bf16[2,8,896,256]{3,2,1,0:T(8,128)(2,1)}) conditional(s32[]{:T(128)} %clamp.3, (bf16[2,896,2048]{2,1,0:T(8,128)(2,1)}, bf16[2,8,7168]{2,1,0:T(8,128)(2,1)}, bf16[2,64,256]{2,1,0:T(8,128)(2,1)}, f32[2,8,128]{2,1,0:T(8,128)S(1)}) %tuple.22, (bf16[2,896,2048]{2,1,0:T(8,128)(2,1)}, ...), branch_computations={%region_0.1_spmd, %region_1.2_spmd, %region_2.3_spmd, %region_3.4_... | conditional | bytes 8 | solution.py:208
  1.4 177.3 %exchange_2.1 = bf16[2,8,896,256]{3,2,1,0:T(8,128)(2,1)} custom-call(bf16[2,896,2048]{2,1,0:T(8,128)(2,1)} %get-tuple-element.50.base, bf16[2,8,7168]{2,1,0:T(8,128)(2,1)} %get-tuple-element.51.left, bf16[2,64,256]{2,1,0:T(8,128)(2,1)} %get-tuple-element.52.right, f32[2,8,128]{2,1,0:T(8,128)S(1)} %get-tuple-element.53.scale), custom_call_target="tpu_custom_call" | custom-call | tf_op jit(solution)/shard_map/cond/branch_2_fun/exchange_2/pallas_call | solution.py:153
  178.7 6.0 %copy_out.1 = bf16[2,7168,256]{2,1,0:T(8,128)(2,1)} custom-call(bf16[2,7168,256]{2,1,0:T(8,128)(2,1)} %bitcast.4), custom_call_target="tpu_custom_call" | custom-call | tf_op jit(solution)/shard_map/copy_out/pallas_call | solution.py:193
